TPU v7x, 16 devices: a whole 2x2x2 slice. The times are simulated.
16 devices in a mesh: tp: 2 (over z), cp: 8 (over y, x, core).
Axes of the slice: x: 2, y: 2, z: 2, core: 2. Of those that a mesh axis runs over, the one named last changes fastest.
Arguments:
- query: bfloat16 [16, 1024, 64, 128], P(None, 'cp', 'tp'), parts along dimension 2
- keys: bfloat16 [16, 1024, 8, 128], P(None, 'cp', 'tp'), parts along dimension 2
- values: bfloat16 [16, 1024, 8, 128], P(None, 'cp', 'tp'), parts along dimension 2
- positions: int32 [16, 1024], P(None, 'cp')
- grad_out: bfloat16 [16, 1024, 64, 128], P(None, 'cp', 'tp'), parts along dimension 2
Outputs:
- output 1: bfloat16 [16, 1024, 64, 128], P(None, 'cp', 'tp'), parts along dimension 2
- output 2: bfloat16 [16, 1024, 64, 128], P(None, 'cp', 'tp'), parts along dimension 2
- output 3: bfloat16 [16, 1024, 8, 128], P(None, 'cp', 'tp'), parts along dimension 2
- output 4: bfloat16 [16, 1024, 8, 128], P(None, 'cp', 'tp'), parts along dimension 2
There are 2 independent parts. A program takes and returns all parts, laid end to end along the dimension named above; an argument that names none is the same for every part.
All inputs are finite; a program needn't handle non-finite values.
Results may differ from a plain program's by a relative error of at most 0.00828705.
Values are sent between devices in bfloat16 or wider.
A program may use at most 1 GiB of HBM per device.

v0:
```python
import jax
import jax.numpy as jnp
from jax import lax
from jax.sharding import PartitionSpec as P

ROPE_THETA = 1000000.0


def rotary(tensor, positions, angle_sign):
    half_dim = tensor.shape[-1] // 2
    freq_expo = jnp.arange(half_dim, dtype=jnp.float32) * (2.0 / tensor.shape[-1])
    inv_freq = 1.0 / (ROPE_THETA ** freq_expo)
    angles = positions.astype(jnp.float32)[:, :, None] * inv_freq
    cosine = jnp.cos(angles)[:, :, None, :]
    sine_val = angle_sign * jnp.sin(angles)[:, :, None, :]
    pairs = tensor.astype(jnp.float32).reshape(tensor.shape[:-1] + (half_dim, 2))
    even_part = pairs[..., 0]
    odd_part = pairs[..., 1]
    new_even = even_part * cosine - odd_part * sine_val
    new_odd = even_part * sine_val + odd_part * cosine
    return jnp.stack([new_even, new_odd], axis=-1).reshape(tensor.shape)


def visibility(q_pos, k_pos):
    return k_pos[:, None, None, None, :] <= q_pos[:, None, None, :, None]


def attend_block(state, q_part, k_part, v_part, score_scale, visible):
    row_max, row_sum, out_acc = state
    scores = jnp.einsum('bqhgd,bkhd->bhgqk', q_part, k_part, preferred_element_type=jnp.float32) * score_scale
    if visible is not None:
        scores = jnp.where(visible, scores, -jnp.inf)
    new_max = jnp.maximum(row_max, jnp.max(scores, axis=-1))
    factor = jnp.exp(row_max - new_max)
    weights = jnp.exp(scores - new_max[..., None])
    row_sum = row_sum * factor + jnp.sum(weights, axis=-1)
    out_acc = out_acc * factor[..., None] + jnp.einsum(
        'bhgqk,bkhd->bhgqd', weights.astype(jnp.bfloat16), v_part, preferred_element_type=jnp.float32)
    return new_max, row_sum, out_acc


def grad_block(q_part, g_part, log_norm, delta_part, k_part, v_part, score_scale, visible):
    scores = jnp.einsum('bqhgd,bkhd->bhgqk', q_part, k_part, preferred_element_type=jnp.float32) * score_scale
    if visible is not None:
        scores = jnp.where(visible, scores, -jnp.inf)
    weights = jnp.exp(scores - log_norm[..., None])
    grad_weights = jnp.einsum('bqhgd,bkhd->bhgqk', g_part, v_part, preferred_element_type=jnp.float32)
    grad_scores = (weights * (grad_weights - delta_part[..., None]) * score_scale).astype(jnp.bfloat16)
    dq_part = jnp.einsum('bhgqk,bkhd->bhgqd', grad_scores, k_part, preferred_element_type=jnp.float32)
    dk_part = jnp.einsum('bhgqk,bqhgd->bkhd', grad_scores, q_part, preferred_element_type=jnp.float32)
    dv_part = jnp.einsum('bhgqk,bqhgd->bkhd', weights.astype(jnp.bfloat16), g_part, preferred_element_type=jnp.float32)
    return dq_part, dk_part, dv_part


def solution(mesh):
    cp_size = mesh.shape['cp']
    shift_pairs = [(src, (src + 1) % cp_size) for src in range(cp_size)]
    head_spec = P(None, 'cp', 'tp', None)
    pos_spec = P(None, 'cp')

    def local_step(query, keys, values, positions, grad_out):
        batch_size, length, n_heads, head_dim = query.shape
        n_kv = keys.shape[2]
        group_size = n_heads // n_kv
        half_len = length // 2
        score_scale = head_dim ** -0.5
        my_index = lax.axis_index('cp')
        q_rot = rotary(query, positions, 1.0).astype(jnp.bfloat16).reshape(batch_size, length, n_kv, group_size, head_dim)
        k_rot = rotary(keys, positions, 1.0).astype(jnp.bfloat16)
        g_grp = grad_out.reshape(batch_size, length, n_kv, group_size, head_dim)
        q_first = q_rot[:, :half_len]
        q_second = q_rot[:, half_len:]
        g_first = g_grp[:, :half_len]
        g_second = g_grp[:, half_len:]
        mask_first = visibility(positions[:, :half_len], positions[:, :half_len])
        mask_second = visibility(positions[:, half_len:], positions)
        row_shape = (batch_size, n_kv, group_size, half_len)
        empty_state = (jnp.full(row_shape, -jnp.inf, jnp.float32), jnp.zeros(row_shape, jnp.float32),
                       jnp.zeros(row_shape + (head_dim,), jnp.float32))
        first_state = attend_block(empty_state, q_first, k_rot[:, :half_len], values[:, :half_len], score_scale, mask_first)
        second_state = attend_block(empty_state, q_second, k_rot, values, score_scale, mask_second)

        def forward_step(step, loop_state):
            kv_buf, first_acc, second_acc = loop_state
            kv_buf = lax.ppermute(kv_buf, 'cp', shift_pairs)
            k_buf, v_buf = kv_buf
            k_lead = k_buf[:, :half_len]
            v_lead = v_buf[:, :half_len]

            def from_before(states):
                return (attend_block(states[0], q_first, k_lead, v_lead, score_scale, None),
                        attend_block(states[1], q_second, k_lead, v_lead, score_scale, None))

            def from_after(states):
                return (states[0], attend_block(states[1], q_second, k_buf, v_buf, score_scale, None))

            source = (my_index - step) % cp_size
            first_acc, second_acc = lax.cond(source < my_index, from_before, from_after, (first_acc, second_acc))
            return kv_buf, first_acc, second_acc

        _, first_state, second_state = lax.fori_loop(
            1, cp_size, forward_step, ((k_rot, values), first_state, second_state))

        out_first = first_state[2] / first_state[1][..., None]
        out_second = second_state[2] / second_state[1][..., None]
        norm_first = first_state[0] + jnp.log(first_state[1])
        norm_second = second_state[0] + jnp.log(second_state[1])
        attn_grp = jnp.concatenate([out_first, out_second], axis=3).astype(jnp.bfloat16).transpose(0, 3, 1, 2, 4)
        attn_out = attn_grp.reshape(batch_size, length, n_heads, head_dim)
        row_delta = jnp.einsum('bqhgd,bqhgd->bhgq', g_grp, attn_grp, preferred_element_type=jnp.float32)
        delta_first = row_delta[..., :half_len]
        delta_second = row_delta[..., half_len:]

        dq_first, dk_lead, dv_lead = grad_block(
            q_first, g_first, norm_first, delta_first, k_rot[:, :half_len], values[:, :half_len], score_scale, mask_first)
        dq_second, dk_own, dv_own = grad_block(
            q_second, g_second, norm_second, delta_second, k_rot, values, score_scale, mask_second)
        dk_acc = jnp.concatenate([dk_own[:, :half_len] + dk_lead, dk_own[:, half_len:]], axis=1)
        dv_acc = jnp.concatenate([dv_own[:, :half_len] + dv_lead, dv_own[:, half_len:]], axis=1)

        def backward_step(step, loop_state):
            kv_buf, dkv_buf, dq_pair = loop_state
            kv_buf, dkv_buf = lax.ppermute((kv_buf, dkv_buf), 'cp', shift_pairs)
            k_buf, v_buf = kv_buf
            k_lead = k_buf[:, :half_len]
            v_lead = v_buf[:, :half_len]

            def from_before(operands):
                dkv_in, dq_in = operands
                grads_a = grad_block(q_first, g_first, norm_first, delta_first, k_lead, v_lead, score_scale, None)
                grads_b = grad_block(q_second, g_second, norm_second, delta_second, k_lead, v_lead, score_scale, None)
                dk_new = jnp.concatenate([dkv_in[0][:, :half_len] + grads_a[1] + grads_b[1], dkv_in[0][:, half_len:]], axis=1)
                dv_new = jnp.concatenate([dkv_in[1][:, :half_len] + grads_a[2] + grads_b[2], dkv_in[1][:, half_len:]], axis=1)
                return (dk_new, dv_new), (dq_in[0] + grads_a[0], dq_in[1] + grads_b[0])

            def from_after(operands):
                dkv_in, dq_in = operands
                grads_b = grad_block(q_second, g_second, norm_second, delta_second, k_buf, v_buf, score_scale, None)
                return (dkv_in[0] + grads_b[1], dkv_in[1] + grads_b[2]), (dq_in[0], dq_in[1] + grads_b[0])

            source = (my_index - step) % cp_size
            dkv_buf, dq_pair = lax.cond(source < my_index, from_before, from_after, (dkv_buf, dq_pair))
            return kv_buf, dkv_buf, dq_pair

        _, dkv_buf, dq_pair = lax.fori_loop(
            1, cp_size, backward_step, ((k_rot, values), (dk_acc, dv_acc), (dq_first, dq_second)))
        dk_rot, dv_sum = lax.ppermute(dkv_buf, 'cp', shift_pairs)

        dq_rot = jnp.concatenate(dq_pair, axis=3).transpose(0, 3, 1, 2, 4).reshape(batch_size, length, n_heads, head_dim)
        grad_query = rotary(dq_rot, positions, -1.0).astype(jnp.bfloat16)
        grad_keys = rotary(dk_rot, positions, -1.0).astype(jnp.bfloat16)
        grad_values = dv_sum.astype(jnp.bfloat16)
        return attn_out, grad_query, grad_keys, grad_values

    return jax.shard_map(local_step, mesh=mesh,
                         in_specs=(head_spec, head_spec, head_spec, pos_spec, head_spec),
                         out_specs=(head_spec, head_spec, head_spec, head_spec), check_vma=False)
```

profile of v0, /device:TPU:13, one launch (start us, length us, event | category | flops | bytes accessed | tf_op | source)
XLA Modules:
  0.0 3783.6 jit_solution(13837484212175172530)
XLA Ops:
  6.3 25.3 copy.35
  140.6 34.0 fusion.128
  262.2 1023.6 %while.54 = (s32[]{:T(128)}, bf16[16,128,4,128]{3,1,2,0:T(8,128)(2,1)}, bf16[16,128,4,128]{3,1,2,0:T(8,128)(2,1)S(1)}, f32[16,4,8,64]{3,2,1,0:T(8,128)S(1)}, f32...) while((s32[]{:T(128)}, ...), condition=%wide.region_13.14_spmd, body=%wide.region_4.13_spmd.sunk | while | flops 2197946368 | bytes 227672784 | solution.py:101
  285.0 22.9 collective-permute-done
  307.9 22.5 collective-permute-done.1
  330.4 96.7 %conditional.4 = (f32[16,4,8,64]{3,2,1,0:T(8,128)S(1)}, f32[16,4,8,64]{3,2,1,0:T(8,128)}, f32[16,4,8,64,128]{4,3,2,1,0:T(8,128)}, f32[16,4,8,64]{3,2,1,0:T(8,128...) conditional(s32[]{:T(128)} %convert_element_type.141, (bf16[16,128,4,128]{3,1,2,0:T(8,128)(2,1)}, ...), branch_computations={%region_5.7_spmd, %region_8.12_spmd} | conditional | flops 2197946368 | bytes 202244304 | solution.py:98
  434.4 22.9 collective-permute-done
  457.4 22.5 collective-permute-done.1
  479.9 96.7 %conditional.4 = (f32[16,4,8,64]{3,2,1,0:T(8,128)S(1)}, f32[16,4,8,64]{3,2,1,0:T(8,128)}, f32[16,4,8,64,128]{4,3,2,1,0:T(8,128)}, f32[16,4,8,64]{3,2,1,0:T(8,128...) conditional(s32[]{:T(128)} %convert_element_type.141, (bf16[16,128,4,128]{3,1,2,0:T(8,128)(2,1)}, ...), branch_computations={%region_5.7_spmd, %region_8.12_spmd} | conditional | flops 2197946368 | bytes 202244304 | solution.py:98
  583.9 22.9 collective-permute-done
  606.8 22.5 collective-permute-done.1
  629.3 96.7 %conditional.4 = (f32[16,4,8,64]{3,2,1,0:T(8,128)S(1)}, f32[16,4,8,64]{3,2,1,0:T(8,128)}, f32[16,4,8,64,128]{4,3,2,1,0:T(8,128)}, f32[16,4,8,64]{3,2,1,0:T(8,128...) conditional(s32[]{:T(128)} %convert_element_type.141, (bf16[16,128,4,128]{3,1,2,0:T(8,128)(2,1)}, ...), branch_computations={%region_5.7_spmd, %region_8.12_spmd} | conditional | flops 2197946368 | bytes 202244304 | solution.py:98
  733.4 22.9 collective-permute-done
  756.3 22.5 collective-permute-done.1
  778.8 96.7 %conditional.4 = (f32[16,4,8,64]{3,2,1,0:T(8,128)S(1)}, f32[16,4,8,64]{3,2,1,0:T(8,128)}, f32[16,4,8,64,128]{4,3,2,1,0:T(8,128)}, f32[16,4,8,64]{3,2,1,0:T(8,128...) conditional(s32[]{:T(128)} %convert_element_type.141, (bf16[16,128,4,128]{3,1,2,0:T(8,128)(2,1)}, ...), branch_computations={%region_5.7_spmd, %region_8.12_spmd} | conditional | flops 2197946368 | bytes 202244304 | solution.py:98
  882.8 22.9 collective-permute-done
  928.2 96.7 %conditional.4 = (f32[16,4,8,64]{3,2,1,0:T(8,128)S(1)}, f32[16,4,8,64]{3,2,1,0:T(8,128)}, f32[16,4,8,64,128]{4,3,2,1,0:T(8,128)}, f32[16,4,8,64]{3,2,1,0:T(8,128...) conditional(s32[]{:T(128)} %convert_element_type.141, (bf16[16,128,4,128]{3,1,2,0:T(8,128)(2,1)}, ...), branch_computations={%region_5.7_spmd, %region_8.12_spmd} | conditional | flops 2197946368 | bytes 202244304 | solution.py:98
  1032.3 22.9 collective-permute-done
  1077.7 45.5 %conditional.4 = (f32[16,4,8,64]{3,2,1,0:T(8,128)S(1)}, f32[16,4,8,64]{3,2,1,0:T(8,128)}, f32[16,4,8,64,128]{4,3,2,1,0:T(8,128)}, f32[16,4,8,64]{3,2,1,0:T(8,128...) conditional(s32[]{:T(128)} %convert_element_type.141, (bf16[16,128,4,128]{3,1,2,0:T(8,128)(2,1)}, ...), branch_computations={%region_5.7_spmd, %region_8.12_spmd} | conditional | flops 2197946368 | bytes 202244304 | solution.py:98
  1127.9 53.8 %collective-permute-start = (bf16[16,128,4,128]{3,1,2,0:T(8,128)(2,1)}, bf16[16,128,4,128]{3,1,2,0:T(8,128)(2,1)}, u32[]{:S(2)}, u32[]{:S(2)}) collective-permute-start(bf16[16,128,4,128]{3,1,2,0:T(8,128)(2,1)} %get-tuple-element.1265), channel_id=1, source_target_pairs={{0,1},{1,2},{2,3},{3,4},{4,5},{5,6},{6,7},{7,0},{8,9},{9,10},{10,1... | collective-permute-start | bytes 6291464 | tf_op jit(solution)/shard_map/while/body/eval_jaxpr/ppermute | solution.py:85
  1181.7 22.9 collective-permute-done
  1227.1 45.5 %conditional.4 = (f32[16,4,8,64]{3,2,1,0:T(8,128)S(1)}, f32[16,4,8,64]{3,2,1,0:T(8,128)}, f32[16,4,8,64,128]{4,3,2,1,0:T(8,128)}, f32[16,4,8,64]{3,2,1,0:T(8,128...) conditional(s32[]{:T(128)} %convert_element_type.141, (bf16[16,128,4,128]{3,1,2,0:T(8,128)(2,1)}, ...), branch_computations={%region_5.7_spmd, %region_8.12_spmd} | conditional | flops 2197946368 | bytes 202244304 | solution.py:98
  1441.2 2039.4 %while.55 = (s32[]{:T(128)}, bf16[16,128,4,128]{3,1,2,0:T(8,128)(2,1)}, bf16[16,128,4,128]{3,1,2,0:T(8,128)(2,1)}, f32[16,128,4,128]{3,1,2,0:T(8,128)}, f32[16,1...) while((s32[]{:T(128)}, ...), condition=%wide.region_17.18_spmd, body=%wide.region_14.17_spmd.sunk | while | flops 5419040768 | bytes 351404768 | solution.py:145
  1444.2 34.3 collective-permute-start.5
  1478.6 78.4 %collective-permute-done.2 = bf16[16,128,4,128]{3,1,2,0:T(8,128)(2,1)S(1)} collective-permute-done((bf16[16,128,4,128]{3,1,2,0:T(8,128)(2,1)}, bf16[16,128,4,128]{3,1,2,0:T(8,128)(2,1)S(1)}, u32[]{:S(2)}, u32[]{:S(2)}) %collective-permute-start.2) | collective-permute-done | bytes 2097184 | tf_op jit(solution)/shard_map/while/body/eval_jaxpr/ppermute | solution.py:123
  1582.7 151.9 %conditional.5 = (f32[16,128,4,128]{3,1,2,0:T(8,128)}, f32[16,128,4,128]{3,1,2,0:T(8,128)}, f32[16,4,8,64,128]{4,3,2,1,0:T(8,128)}, f32[16,4,8,64,128]{4,3,2,1,0:T(8,128)}) conditional(s32[]{:T(128)} %convert_element_type.142, (bf16[16,128,4,128]{3,1,2,0:T(8,128)(2,1)S(1)}, bf16[16,64,4,8,128]{4,1,3,2,0:T(8,128)(2,1)}, ...), branch_computations={%region_15.15_spmd, %region_16.16_spmd} | conditional | flops 5419040768 | bytes 292683872 | solution.py:142
  1744.5 31.9 collective-permute-start.5
  1776.5 80.9 %collective-permute-done.2 = bf16[16,128,4,128]{3,1,2,0:T(8,128)(2,1)S(1)} collective-permute-done((bf16[16,128,4,128]{3,1,2,0:T(8,128)(2,1)}, bf16[16,128,4,128]{3,1,2,0:T(8,128)(2,1)S(1)}, u32[]{:S(2)}, u32[]{:S(2)}) %collective-permute-start.2) | collective-permute-done | bytes 2097184 | tf_op jit(solution)/shard_map/while/body/eval_jaxpr/ppermute | solution.py:123
  1883.0 151.9 %conditional.5 = (f32[16,128,4,128]{3,1,2,0:T(8,128)}, f32[16,128,4,128]{3,1,2,0:T(8,128)}, f32[16,4,8,64,128]{4,3,2,1,0:T(8,128)}, f32[16,4,8,64,128]{4,3,2,1,0:T(8,128)}) conditional(s32[]{:T(128)} %convert_element_type.142, (bf16[16,128,4,128]{3,1,2,0:T(8,128)(2,1)S(1)}, bf16[16,64,4,8,128]{4,1,3,2,0:T(8,128)(2,1)}, ...), branch_computations={%region_15.15_spmd, %region_16.16_spmd} | conditional | flops 5419040768 | bytes 292683872 | solution.py:142
  2045.0 29.4 collective-permute-start.5
  2074.4 83.4 %collective-permute-done.2 = bf16[16,128,4,128]{3,1,2,0:T(8,128)(2,1)S(1)} collective-permute-done((bf16[16,128,4,128]{3,1,2,0:T(8,128)(2,1)}, bf16[16,128,4,128]{3,1,2,0:T(8,128)(2,1)S(1)}, u32[]{:S(2)}, u32[]{:S(2)}) %collective-permute-start.2) | collective-permute-done | bytes 2097184 | tf_op jit(solution)/shard_map/while/body/eval_jaxpr/ppermute | solution.py:123
  2183.5 162.7 %conditional.5 = (f32[16,128,4,128]{3,1,2,0:T(8,128)}, f32[16,128,4,128]{3,1,2,0:T(8,128)}, f32[16,4,8,64,128]{4,3,2,1,0:T(8,128)}, f32[16,4,8,64,128]{4,3,2,1,0:T(8,128)}) conditional(s32[]{:T(128)} %convert_element_type.142, (bf16[16,128,4,128]{3,1,2,0:T(8,128)(2,1)S(1)}, bf16[16,64,4,8,128]{4,1,3,2,0:T(8,128)(2,1)}, ...), branch_computations={%region_15.15_spmd, %region_16.16_spmd} | conditional | flops 5419040768 | bytes 292683872 | solution.py:142
  2356.1 26.9 collective-permute-start.5
  2383.0 85.9 %collective-permute-done.2 = bf16[16,128,4,128]{3,1,2,0:T(8,128)(2,1)S(1)} collective-permute-done((bf16[16,128,4,128]{3,1,2,0:T(8,128)(2,1)}, bf16[16,128,4,128]{3,1,2,0:T(8,128)(2,1)S(1)}, u32[]{:S(2)}, u32[]{:S(2)}) %collective-permute-start.2) | collective-permute-done | bytes 2097184 | tf_op jit(solution)/shard_map/while/body/eval_jaxpr/ppermute | solution.py:123
  2494.6 151.9 %conditional.5 = (f32[16,128,4,128]{3,1,2,0:T(8,128)}, f32[16,128,4,128]{3,1,2,0:T(8,128)}, f32[16,4,8,64,128]{4,3,2,1,0:T(8,128)}, f32[16,4,8,64,128]{4,3,2,1,0:T(8,128)}) conditional(s32[]{:T(128)} %convert_element_type.142, (bf16[16,128,4,128]{3,1,2,0:T(8,128)(2,1)S(1)}, bf16[16,64,4,8,128]{4,1,3,2,0:T(8,128)(2,1)}, ...), branch_computations={%region_15.15_spmd, %region_16.16_spmd} | conditional | flops 5419040768 | bytes 292683872 | solution.py:142
  2656.5 24.4 collective-permute-start.5
  2681.0 88.4 %collective-permute-done.2 = bf16[16,128,4,128]{3,1,2,0:T(8,128)(2,1)S(1)} collective-permute-done((bf16[16,128,4,128]{3,1,2,0:T(8,128)(2,1)}, bf16[16,128,4,128]{3,1,2,0:T(8,128)(2,1)S(1)}, u32[]{:S(2)}, u32[]{:S(2)}) %collective-permute-start.2) | collective-permute-done | bytes 2097184 | tf_op jit(solution)/shard_map/while/body/eval_jaxpr/ppermute | solution.py:123
  2795.0 162.7 %conditional.5 = (f32[16,128,4,128]{3,1,2,0:T(8,128)}, f32[16,128,4,128]{3,1,2,0:T(8,128)}, f32[16,4,8,64,128]{4,3,2,1,0:T(8,128)}, f32[16,4,8,64,128]{4,3,2,1,0:T(8,128)}) conditional(s32[]{:T(128)} %convert_element_type.142, (bf16[16,128,4,128]{3,1,2,0:T(8,128)(2,1)S(1)}, bf16[16,64,4,8,128]{4,1,3,2,0:T(8,128)(2,1)}, ...), branch_computations={%region_15.15_spmd, %region_16.16_spmd} | conditional | flops 5419040768 | bytes 292683872 | solution.py:142
  2989.6 90.9 %collective-permute-done.2 = bf16[16,128,4,128]{3,1,2,0:T(8,128)(2,1)S(1)} collective-permute-done((bf16[16,128,4,128]{3,1,2,0:T(8,128)(2,1)}, bf16[16,128,4,128]{3,1,2,0:T(8,128)(2,1)S(1)}, u32[]{:S(2)}, u32[]{:S(2)}) %collective-permute-start.2) | collective-permute-done | bytes 2097184 | tf_op jit(solution)/shard_map/while/body/eval_jaxpr/ppermute | solution.py:123
  3106.1 65.3 %conditional.5 = (f32[16,128,4,128]{3,1,2,0:T(8,128)}, f32[16,128,4,128]{3,1,2,0:T(8,128)}, f32[16,4,8,64,128]{4,3,2,1,0:T(8,128)}, f32[16,4,8,64,128]{4,3,2,1,0:T(8,128)}) conditional(s32[]{:T(128)} %convert_element_type.142, (bf16[16,128,4,128]{3,1,2,0:T(8,128)(2,1)S(1)}, bf16[16,64,4,8,128]{4,1,3,2,0:T(8,128)(2,1)}, ...), branch_computations={%region_15.15_spmd, %region_16.16_spmd} | conditional | flops 5419040768 | bytes 292683872 | solution.py:142
  3171.6 96.5 %collective-permute-start.4 = (f32[16,128,4,128]{3,1,2,0:T(8,128)}, f32[16,128,4,128]{3,1,2,0:T(8,128)}, u32[]{:S(2)}, u32[]{:S(2)}) collective-permute-start(f32[16,128,4,128]{3,1,2,0:T(8,128)} %get-tuple-element.1319), channel_id=1, source_target_pairs={{0,1},{1,2},{2,3},{3,4},{4,5},{5,6},{6,7},{7,0},{8,9},{9,10},{10,1... | collective-permute-start | bytes 12582920 | tf_op jit(solution)/shard_map/while/body/eval_jaxpr/ppermute | solution.py:123
  3287.6 93.3 %collective-permute-done.2 = bf16[16,128,4,128]{3,1,2,0:T(8,128)(2,1)S(1)} collective-permute-done((bf16[16,128,4,128]{3,1,2,0:T(8,128)(2,1)}, bf16[16,128,4,128]{3,1,2,0:T(8,128)(2,1)S(1)}, u32[]{:S(2)}, u32[]{:S(2)}) %collective-permute-start.2) | collective-permute-done | bytes 2097184 | tf_op jit(solution)/shard_map/while/body/eval_jaxpr/ppermute | solution.py:123
  3406.6 64.3 %conditional.5 = (f32[16,128,4,128]{3,1,2,0:T(8,128)}, f32[16,128,4,128]{3,1,2,0:T(8,128)}, f32[16,4,8,64,128]{4,3,2,1,0:T(8,128)}, f32[16,4,8,64,128]{4,3,2,1,0:T(8,128)}) conditional(s32[]{:T(128)} %convert_element_type.142, (bf16[16,128,4,128]{3,1,2,0:T(8,128)(2,1)S(1)}, bf16[16,64,4,8,128]{4,1,3,2,0:T(8,128)(2,1)}, ...), branch_computations={%region_15.15_spmd, %region_16.16_spmd} | conditional | flops 5419040768 | bytes 292683872 | solution.py:142
  3493.2 122.7 %collective-permute-start.7 = (bf16[16,128,4,128]{3,2,1,0:T(4,128)(2,1)S(1)}, bf16[16,128,4,128]{3,2,1,0:T(4,128)(2,1)}, u32[]{:S(2)}, u32[]{:S(2)}) collective-permute-start(bf16[16,128,4,128]{3,2,1,0:T(4,128)(2,1)S(1)} %copy.57), channel_id=1, source_target_pairs={{0,1},{1,2},{2,3},{3,4},{4,5},{5,6},{6,7},{7,0},{8,9},{9,10},{10,1... | collective-permute-start | bytes 6291464 | tf_op jit(solution)/shard_map/ppermute | solution.py:147
  3615.9 30.4 copy.53
  3646.3 30.4 copy.54
  3676.8 32.7 pad_maximum_fusion.2
  3728.8 25.3 copy.58
  (437 shorter events, 2229.6 us)
Async XLA Ops:
  5.2 99.8 %copy-start.20 = (f32[16,128,64]{1,0,2:T(8,128)}, f32[16,128,64]{1,0,2:T(8,128)S(1)}, u32[]{:S(2)}) copy-start(f32[16,128,64]{1,0,2:T(8,128)S(1)} %get-tuple-element.1029) | copy-start | bytes 1572868
  5.3 45.2 %copy-start.22 = (f32[16,128,64]{1,2,0:T(8,128)}, f32[16,128,64]{1,2,0:T(8,128)S(1)}, u32[]{:S(2)}) copy-start(f32[16,128,64]{1,2,0:T(8,128)S(1)} %copy.36) | copy-start | bytes 1572868
  133.4 52.1 %copy-start.9 = (bf16[16,128,4,128,1]{3,1,4,2,0:T(8,128)(2,1)}, bf16[16,128,4,128,1]{3,1,4,2,0:T(8,128)(2,1)S(1)}, u32[]{:S(2)}) copy-start(bf16[16,128,4,128,1]{3,1,4,2,0:T(8,128)(2,1)S(1)} %copy.81) | copy-start | bytes 6291460
  283.1 24.8 collective-permute-start
  285.0 45.4 %collective-permute-start.1 = (bf16[16,128,4,128]{3,1,2,0:T(8,128)(2,1)S(1)}, bf16[16,128,4,128]{3,1,2,0:T(8,128)(2,1)}, u32[]{:S(2)}, u32[]{:S(2)}) collective-permute-start(bf16[16,128,4,128]{3,1,2,0:T(8,128)(2,1)S(1)} %get-tuple-element.1266), channel_id=1, source_target_pairs={{0,1},{1,2},{2,3},{3,4},{4,5},{5,6},{6,7},{7,0},{8,9},{9,10},{10,1... | collective-permute-start | bytes 6291464 | tf_op jit(solution)/shard_map/while/body/eval_jaxpr/ppermute | solution.py:85
  431.9 25.5 collective-permute-start
  434.4 45.4 %collective-permute-start.1 = (bf16[16,128,4,128]{3,1,2,0:T(8,128)(2,1)S(1)}, bf16[16,128,4,128]{3,1,2,0:T(8,128)(2,1)}, u32[]{:S(2)}, u32[]{:S(2)}) collective-permute-start(bf16[16,128,4,128]{3,1,2,0:T(8,128)(2,1)S(1)} %get-tuple-element.1266), channel_id=1, source_target_pairs={{0,1},{1,2},{2,3},{3,4},{4,5},{5,6},{6,7},{7,0},{8,9},{9,10},{10,1... | collective-permute-start | bytes 6291464 | tf_op jit(solution)/shard_map/while/body/eval_jaxpr/ppermute | solution.py:85
  581.4 25.5 collective-permute-start
  583.9 45.4 %collective-permute-start.1 = (bf16[16,128,4,128]{3,1,2,0:T(8,128)(2,1)S(1)}, bf16[16,128,4,128]{3,1,2,0:T(8,128)(2,1)}, u32[]{:S(2)}, u32[]{:S(2)}) collective-permute-start(bf16[16,128,4,128]{3,1,2,0:T(8,128)(2,1)S(1)} %get-tuple-element.1266), channel_id=1, source_target_pairs={{0,1},{1,2},{2,3},{3,4},{4,5},{5,6},{6,7},{7,0},{8,9},{9,10},{10,1... | collective-permute-start | bytes 6291464 | tf_op jit(solution)/shard_map/while/body/eval_jaxpr/ppermute | solution.py:85
  730.8 25.5 collective-permute-start
  733.3 45.4 %collective-permute-start.1 = (bf16[16,128,4,128]{3,1,2,0:T(8,128)(2,1)S(1)}, bf16[16,128,4,128]{3,1,2,0:T(8,128)(2,1)}, u32[]{:S(2)}, u32[]{:S(2)}) collective-permute-start(bf16[16,128,4,128]{3,1,2,0:T(8,128)(2,1)S(1)} %get-tuple-element.1266), channel_id=1, source_target_pairs={{0,1},{1,2},{2,3},{3,4},{4,5},{5,6},{6,7},{7,0},{8,9},{9,10},{10,1... | collective-permute-start | bytes 6291464 | tf_op jit(solution)/shard_map/while/body/eval_jaxpr/ppermute | solution.py:85
  880.3 25.5 collective-permute-start
  882.8 45.4 %collective-permute-start.1 = (bf16[16,128,4,128]{3,1,2,0:T(8,128)(2,1)S(1)}, bf16[16,128,4,128]{3,1,2,0:T(8,128)(2,1)}, u32[]{:S(2)}, u32[]{:S(2)}) collective-permute-start(bf16[16,128,4,128]{3,1,2,0:T(8,128)(2,1)S(1)} %get-tuple-element.1266), channel_id=1, source_target_pairs={{0,1},{1,2},{2,3},{3,4},{4,5},{5,6},{6,7},{7,0},{8,9},{9,10},{10,1... | collective-permute-start | bytes 6291464 | tf_op jit(solution)/shard_map/while/body/eval_jaxpr/ppermute | solution.py:85
  1029.7 25.5 collective-permute-start
  1032.3 45.4 %collective-permute-start.1 = (bf16[16,128,4,128]{3,1,2,0:T(8,128)(2,1)S(1)}, bf16[16,128,4,128]{3,1,2,0:T(8,128)(2,1)}, u32[]{:S(2)}, u32[]{:S(2)}) collective-permute-start(bf16[16,128,4,128]{3,1,2,0:T(8,128)(2,1)S(1)} %get-tuple-element.1266), channel_id=1, source_target_pairs={{0,1},{1,2},{2,3},{3,4},{4,5},{5,6},{6,7},{7,0},{8,9},{9,10},{10,1... | collective-permute-start | bytes 6291464 | tf_op jit(solution)/shard_map/while/body/eval_jaxpr/ppermute | solution.py:85
  1127.9 76.7 %collective-permute-start = (bf16[16,128,4,128]{3,1,2,0:T(8,128)(2,1)}, bf16[16,128,4,128]{3,1,2,0:T(8,128)(2,1)}, u32[]{:S(2)}, u32[]{:S(2)}) collective-permute-start(bf16[16,128,4,128]{3,1,2,0:T(8,128)(2,1)} %get-tuple-element.1265), channel_id=1, source_target_pairs={{0,1},{1,2},{2,3},{3,4},{4,5},{5,6},{6,7},{7,0},{8,9},{9,10},{10,1... | collective-permute-start | bytes 6291464 | tf_op jit(solution)/shard_map/while/body/eval_jaxpr/ppermute | solution.py:85
  1181.7 45.4 %collective-permute-start.1 = (bf16[16,128,4,128]{3,1,2,0:T(8,128)(2,1)S(1)}, bf16[16,128,4,128]{3,1,2,0:T(8,128)(2,1)}, u32[]{:S(2)}, u32[]{:S(2)}) collective-permute-start(bf16[16,128,4,128]{3,1,2,0:T(8,128)(2,1)S(1)} %get-tuple-element.1266), channel_id=1, source_target_pairs={{0,1},{1,2},{2,3},{3,4},{4,5},{5,6},{6,7},{7,0},{8,9},{9,10},{10,1... | collective-permute-start | bytes 6291464 | tf_op jit(solution)/shard_map/while/body/eval_jaxpr/ppermute | solution.py:85
  1441.6 141.1 %collective-permute-start.4 = (f32[16,128,4,128]{3,1,2,0:T(8,128)}, f32[16,128,4,128]{3,1,2,0:T(8,128)}, u32[]{:S(2)}, u32[]{:S(2)}) collective-permute-start(f32[16,128,4,128]{3,1,2,0:T(8,128)} %get-tuple-element.1319), channel_id=1, source_target_pairs={{0,1},{1,2},{2,3},{3,4},{4,5},{5,6},{6,7},{7,0},{8,9},{9,10},{10,1... | collective-permute-start | bytes 12582920 | tf_op jit(solution)/shard_map/while/body/eval_jaxpr/ppermute | solution.py:123
  1444.2 138.5 %collective-permute-start.5 = (f32[16,128,4,128]{3,1,2,0:T(8,128)}, f32[16,128,4,128]{3,1,2,0:T(8,128)}, u32[]{:S(2)}, u32[]{:S(2)}) collective-permute-start(f32[16,128,4,128]{3,1,2,0:T(8,128)} %get-tuple-element.1320), channel_id=1, source_target_pairs={{0,1},{1,2},{2,3},{3,4},{4,5},{5,6},{6,7},{7,0},{8,9},{9,10},{10,1... | collective-permute-start | bytes 12582920 | tf_op jit(solution)/shard_map/while/body/eval_jaxpr/ppermute | solution.py:123
  1478.5 78.5 %collective-permute-start.2 = (bf16[16,128,4,128]{3,1,2,0:T(8,128)(2,1)}, bf16[16,128,4,128]{3,1,2,0:T(8,128)(2,1)S(1)}, u32[]{:S(2)}, u32[]{:S(2)}) collective-permute-start(bf16[16,128,4,128]{3,1,2,0:T(8,128)(2,1)} %get-tuple-element.1317), channel_id=1, source_target_pairs={{0,1},{1,2},{2,3},{3,4},{4,5},{5,6},{6,7},{7,0},{8,9},{9,10},{10,1... | collective-permute-start | bytes 6291464 | tf_op jit(solution)/shard_map/while/body/eval_jaxpr/ppermute | solution.py:123
  1478.6 100.9 %collective-permute-start.3 = (bf16[16,128,4,128]{3,1,2,0:T(8,128)(2,1)}, bf16[16,128,4,128]{3,1,2,0:T(8,128)(2,1)}, u32[]{:S(2)}, u32[]{:S(2)}) collective-permute-start(bf16[16,128,4,128]{3,1,2,0:T(8,128)(2,1)} %get-tuple-element.1318), channel_id=1, source_target_pairs={{0,1},{1,2},{2,3},{3,4},{4,5},{5,6},{6,7},{7,0},{8,9},{9,10},{10,1... | collective-permute-start | bytes 6291464 | tf_op jit(solution)/shard_map/while/body/eval_jaxpr/ppermute | solution.py:123
  1742.0 141.0 %collective-permute-start.4 = (f32[16,128,4,128]{3,1,2,0:T(8,128)}, f32[16,128,4,128]{3,1,2,0:T(8,128)}, u32[]{:S(2)}, u32[]{:S(2)}) collective-permute-start(f32[16,128,4,128]{3,1,2,0:T(8,128)} %get-tuple-element.1319), channel_id=1, source_target_pairs={{0,1},{1,2},{2,3},{3,4},{4,5},{5,6},{6,7},{7,0},{8,9},{9,10},{10,1... | collective-permute-start | bytes 12582920 | tf_op jit(solution)/shard_map/while/body/eval_jaxpr/ppermute | solution.py:123
  1744.5 138.5 %collective-permute-start.5 = (f32[16,128,4,128]{3,1,2,0:T(8,128)}, f32[16,128,4,128]{3,1,2,0:T(8,128)}, u32[]{:S(2)}, u32[]{:S(2)}) collective-permute-start(f32[16,128,4,128]{3,1,2,0:T(8,128)} %get-tuple-element.1320), channel_id=1, source_target_pairs={{0,1},{1,2},{2,3},{3,4},{4,5},{5,6},{6,7},{7,0},{8,9},{9,10},{10,1... | collective-permute-start | bytes 12582920 | tf_op jit(solution)/shard_map/while/body/eval_jaxpr/ppermute | solution.py:123
  1776.4 81.0 %collective-permute-start.2 = (bf16[16,128,4,128]{3,1,2,0:T(8,128)(2,1)}, bf16[16,128,4,128]{3,1,2,0:T(8,128)(2,1)S(1)}, u32[]{:S(2)}, u32[]{:S(2)}) collective-permute-start(bf16[16,128,4,128]{3,1,2,0:T(8,128)(2,1)} %get-tuple-element.1317), channel_id=1, source_target_pairs={{0,1},{1,2},{2,3},{3,4},{4,5},{5,6},{6,7},{7,0},{8,9},{9,10},{10,1... | collective-permute-start | bytes 6291464 | tf_op jit(solution)/shard_map/while/body/eval_jaxpr/ppermute | solution.py:123
  1776.4 103.4 %collective-permute-start.3 = (bf16[16,128,4,128]{3,1,2,0:T(8,128)(2,1)}, bf16[16,128,4,128]{3,1,2,0:T(8,128)(2,1)}, u32[]{:S(2)}, u32[]{:S(2)}) collective-permute-start(bf16[16,128,4,128]{3,1,2,0:T(8,128)(2,1)} %get-tuple-element.1318), channel_id=1, source_target_pairs={{0,1},{1,2},{2,3},{3,4},{4,5},{5,6},{6,7},{7,0},{8,9},{9,10},{10,1... | collective-permute-start | bytes 6291464 | tf_op jit(solution)/shard_map/while/body/eval_jaxpr/ppermute | solution.py:123
  2042.4 141.0 %collective-permute-start.4 = (f32[16,128,4,128]{3,1,2,0:T(8,128)}, f32[16,128,4,128]{3,1,2,0:T(8,128)}, u32[]{:S(2)}, u32[]{:S(2)}) collective-permute-start(f32[16,128,4,128]{3,1,2,0:T(8,128)} %get-tuple-element.1319), channel_id=1, source_target_pairs={{0,1},{1,2},{2,3},{3,4},{4,5},{5,6},{6,7},{7,0},{8,9},{9,10},{10,1... | collective-permute-start | bytes 12582920 | tf_op jit(solution)/shard_map/while/body/eval_jaxpr/ppermute | solution.py:123
  2045.0 138.5 %collective-permute-start.5 = (f32[16,128,4,128]{3,1,2,0:T(8,128)}, f32[16,128,4,128]{3,1,2,0:T(8,128)}, u32[]{:S(2)}, u32[]{:S(2)}) collective-permute-start(f32[16,128,4,128]{3,1,2,0:T(8,128)} %get-tuple-element.1320), channel_id=1, source_target_pairs={{0,1},{1,2},{2,3},{3,4},{4,5},{5,6},{6,7},{7,0},{8,9},{9,10},{10,1... | collective-permute-start | bytes 12582920 | tf_op jit(solution)/shard_map/while/body/eval_jaxpr/ppermute | solution.py:123
  2074.3 83.5 %collective-permute-start.2 = (bf16[16,128,4,128]{3,1,2,0:T(8,128)(2,1)}, bf16[16,128,4,128]{3,1,2,0:T(8,128)(2,1)S(1)}, u32[]{:S(2)}, u32[]{:S(2)}) collective-permute-start(bf16[16,128,4,128]{3,1,2,0:T(8,128)(2,1)} %get-tuple-element.1317), channel_id=1, source_target_pairs={{0,1},{1,2},{2,3},{3,4},{4,5},{5,6},{6,7},{7,0},{8,9},{9,10},{10,1... | collective-permute-start | bytes 6291464 | tf_op jit(solution)/shard_map/while/body/eval_jaxpr/ppermute | solution.py:123
  2074.4 105.9 %collective-permute-start.3 = (bf16[16,128,4,128]{3,1,2,0:T(8,128)(2,1)}, bf16[16,128,4,128]{3,1,2,0:T(8,128)(2,1)}, u32[]{:S(2)}, u32[]{:S(2)}) collective-permute-start(bf16[16,128,4,128]{3,1,2,0:T(8,128)(2,1)} %get-tuple-element.1318), channel_id=1, source_target_pairs={{0,1},{1,2},{2,3},{3,4},{4,5},{5,6},{6,7},{7,0},{8,9},{9,10},{10,1... | collective-permute-start | bytes 6291464 | tf_op jit(solution)/shard_map/while/body/eval_jaxpr/ppermute | solution.py:123
  2353.5 141.0 %collective-permute-start.4 = (f32[16,128,4,128]{3,1,2,0:T(8,128)}, f32[16,128,4,128]{3,1,2,0:T(8,128)}, u32[]{:S(2)}, u32[]{:S(2)}) collective-permute-start(f32[16,128,4,128]{3,1,2,0:T(8,128)} %get-tuple-element.1319), channel_id=1, source_target_pairs={{0,1},{1,2},{2,3},{3,4},{4,5},{5,6},{6,7},{7,0},{8,9},{9,10},{10,1... | collective-permute-start | bytes 12582920 | tf_op jit(solution)/shard_map/while/body/eval_jaxpr/ppermute | solution.py:123
  2356.1 138.5 %collective-permute-start.5 = (f32[16,128,4,128]{3,1,2,0:T(8,128)}, f32[16,128,4,128]{3,1,2,0:T(8,128)}, u32[]{:S(2)}, u32[]{:S(2)}) collective-permute-start(f32[16,128,4,128]{3,1,2,0:T(8,128)} %get-tuple-element.1320), channel_id=1, source_target_pairs={{0,1},{1,2},{2,3},{3,4},{4,5},{5,6},{6,7},{7,0},{8,9},{9,10},{10,1... | collective-permute-start | bytes 12582920 | tf_op jit(solution)/shard_map/while/body/eval_jaxpr/ppermute | solution.py:123
  2382.9 86.0 %collective-permute-start.2 = (bf16[16,128,4,128]{3,1,2,0:T(8,128)(2,1)}, bf16[16,128,4,128]{3,1,2,0:T(8,128)(2,1)S(1)}, u32[]{:S(2)}, u32[]{:S(2)}) collective-permute-start(bf16[16,128,4,128]{3,1,2,0:T(8,128)(2,1)} %get-tuple-element.1317), channel_id=1, source_target_pairs={{0,1},{1,2},{2,3},{3,4},{4,5},{5,6},{6,7},{7,0},{8,9},{9,10},{10,1... | collective-permute-start | bytes 6291464 | tf_op jit(solution)/shard_map/while/body/eval_jaxpr/ppermute | solution.py:123
  2383.0 108.4 %collective-permute-start.3 = (bf16[16,128,4,128]{3,1,2,0:T(8,128)(2,1)}, bf16[16,128,4,128]{3,1,2,0:T(8,128)(2,1)}, u32[]{:S(2)}, u32[]{:S(2)}) collective-permute-start(bf16[16,128,4,128]{3,1,2,0:T(8,128)(2,1)} %get-tuple-element.1318), channel_id=1, source_target_pairs={{0,1},{1,2},{2,3},{3,4},{4,5},{5,6},{6,7},{7,0},{8,9},{9,10},{10,1... | collective-permute-start | bytes 6291464 | tf_op jit(solution)/shard_map/while/body/eval_jaxpr/ppermute | solution.py:123
  2654.0 141.0 %collective-permute-start.4 = (f32[16,128,4,128]{3,1,2,0:T(8,128)}, f32[16,128,4,128]{3,1,2,0:T(8,128)}, u32[]{:S(2)}, u32[]{:S(2)}) collective-permute-start(f32[16,128,4,128]{3,1,2,0:T(8,128)} %get-tuple-element.1319), channel_id=1, source_target_pairs={{0,1},{1,2},{2,3},{3,4},{4,5},{5,6},{6,7},{7,0},{8,9},{9,10},{10,1... | collective-permute-start | bytes 12582920 | tf_op jit(solution)/shard_map/while/body/eval_jaxpr/ppermute | solution.py:123
  2656.5 138.5 %collective-permute-start.5 = (f32[16,128,4,128]{3,1,2,0:T(8,128)}, f32[16,128,4,128]{3,1,2,0:T(8,128)}, u32[]{:S(2)}, u32[]{:S(2)}) collective-permute-start(f32[16,128,4,128]{3,1,2,0:T(8,128)} %get-tuple-element.1320), channel_id=1, source_target_pairs={{0,1},{1,2},{2,3},{3,4},{4,5},{5,6},{6,7},{7,0},{8,9},{9,10},{10,1... | collective-permute-start | bytes 12582920 | tf_op jit(solution)/shard_map/while/body/eval_jaxpr/ppermute | solution.py:123
  2680.9 88.5 %collective-permute-start.2 = (bf16[16,128,4,128]{3,1,2,0:T(8,128)(2,1)}, bf16[16,128,4,128]{3,1,2,0:T(8,128)(2,1)S(1)}, u32[]{:S(2)}, u32[]{:S(2)}) collective-permute-start(bf16[16,128,4,128]{3,1,2,0:T(8,128)(2,1)} %get-tuple-element.1317), channel_id=1, source_target_pairs={{0,1},{1,2},{2,3},{3,4},{4,5},{5,6},{6,7},{7,0},{8,9},{9,10},{10,1... | collective-permute-start | bytes 6291464 | tf_op jit(solution)/shard_map/while/body/eval_jaxpr/ppermute | solution.py:123
  2680.9 110.9 %collective-permute-start.3 = (bf16[16,128,4,128]{3,1,2,0:T(8,128)(2,1)}, bf16[16,128,4,128]{3,1,2,0:T(8,128)(2,1)}, u32[]{:S(2)}, u32[]{:S(2)}) collective-permute-start(bf16[16,128,4,128]{3,1,2,0:T(8,128)(2,1)} %get-tuple-element.1318), channel_id=1, source_target_pairs={{0,1},{1,2},{2,3},{3,4},{4,5},{5,6},{6,7},{7,0},{8,9},{9,10},{10,1... | collective-permute-start | bytes 6291464 | tf_op jit(solution)/shard_map/while/body/eval_jaxpr/ppermute | solution.py:123
  2965.1 141.0 %collective-permute-start.4 = (f32[16,128,4,128]{3,1,2,0:T(8,128)}, f32[16,128,4,128]{3,1,2,0:T(8,128)}, u32[]{:S(2)}, u32[]{:S(2)}) collective-permute-start(f32[16,128,4,128]{3,1,2,0:T(8,128)} %get-tuple-element.1319), channel_id=1, source_target_pairs={{0,1},{1,2},{2,3},{3,4},{4,5},{5,6},{6,7},{7,0},{8,9},{9,10},{10,1... | collective-permute-start | bytes 12582920 | tf_op jit(solution)/shard_map/while/body/eval_jaxpr/ppermute | solution.py:123
  2967.6 138.5 %collective-permute-start.5 = (f32[16,128,4,128]{3,1,2,0:T(8,128)}, f32[16,128,4,128]{3,1,2,0:T(8,128)}, u32[]{:S(2)}, u32[]{:S(2)}) collective-permute-start(f32[16,128,4,128]{3,1,2,0:T(8,128)} %get-tuple-element.1320), channel_id=1, source_target_pairs={{0,1},{1,2},{2,3},{3,4},{4,5},{5,6},{6,7},{7,0},{8,9},{9,10},{10,1... | collective-permute-start | bytes 12582920 | tf_op jit(solution)/shard_map/while/body/eval_jaxpr/ppermute | solution.py:123
  2989.5 91.0 %collective-permute-start.2 = (bf16[16,128,4,128]{3,1,2,0:T(8,128)(2,1)}, bf16[16,128,4,128]{3,1,2,0:T(8,128)(2,1)S(1)}, u32[]{:S(2)}, u32[]{:S(2)}) collective-permute-start(bf16[16,128,4,128]{3,1,2,0:T(8,128)(2,1)} %get-tuple-element.1317), channel_id=1, source_target_pairs={{0,1},{1,2},{2,3},{3,4},{4,5},{5,6},{6,7},{7,0},{8,9},{9,10},{10,1... | collective-permute-start | bytes 6291464 | tf_op jit(solution)/shard_map/while/body/eval_jaxpr/ppermute | solution.py:123
  2989.6 113.4 %collective-permute-start.3 = (bf16[16,128,4,128]{3,1,2,0:T(8,128)(2,1)}, bf16[16,128,4,128]{3,1,2,0:T(8,128)(2,1)}, u32[]{:S(2)}, u32[]{:S(2)}) collective-permute-start(bf16[16,128,4,128]{3,1,2,0:T(8,128)(2,1)} %get-tuple-element.1318), channel_id=1, source_target_pairs={{0,1},{1,2},{2,3},{3,4},{4,5},{5,6},{6,7},{7,0},{8,9},{9,10},{10,1... | collective-permute-start | bytes 6291464 | tf_op jit(solution)/shard_map/while/body/eval_jaxpr/ppermute | solution.py:123
  3171.6 235.0 %collective-permute-start.4 = (f32[16,128,4,128]{3,1,2,0:T(8,128)}, f32[16,128,4,128]{3,1,2,0:T(8,128)}, u32[]{:S(2)}, u32[]{:S(2)}) collective-permute-start(f32[16,128,4,128]{3,1,2,0:T(8,128)} %get-tuple-element.1319), channel_id=1, source_target_pairs={{0,1},{1,2},{2,3},{3,4},{4,5},{5,6},{6,7},{7,0},{8,9},{9,10},{10,1... | collective-permute-start | bytes 12582920 | tf_op jit(solution)/shard_map/while/body/eval_jaxpr/ppermute | solution.py:123
  3268.1 138.5 %collective-permute-start.5 = (f32[16,128,4,128]{3,1,2,0:T(8,128)}, f32[16,128,4,128]{3,1,2,0:T(8,128)}, u32[]{:S(2)}, u32[]{:S(2)}) collective-permute-start(f32[16,128,4,128]{3,1,2,0:T(8,128)} %get-tuple-element.1320), channel_id=1, source_target_pairs={{0,1},{1,2},{2,3},{3,4},{4,5},{5,6},{6,7},{7,0},{8,9},{9,10},{10,1... | collective-permute-start | bytes 12582920 | tf_op jit(solution)/shard_map/while/body/eval_jaxpr/ppermute | solution.py:123
  3287.5 93.5 %collective-permute-start.2 = (bf16[16,128,4,128]{3,1,2,0:T(8,128)(2,1)}, bf16[16,128,4,128]{3,1,2,0:T(8,128)(2,1)S(1)}, u32[]{:S(2)}, u32[]{:S(2)}) collective-permute-start(bf16[16,128,4,128]{3,1,2,0:T(8,128)(2,1)} %get-tuple-element.1317), channel_id=1, source_target_pairs={{0,1},{1,2},{2,3},{3,4},{4,5},{5,6},{6,7},{7,0},{8,9},{9,10},{10,1... | collective-permute-start | bytes 6291464 | tf_op jit(solution)/shard_map/while/body/eval_jaxpr/ppermute | solution.py:123
  3287.5 115.9 %collective-permute-start.3 = (bf16[16,128,4,128]{3,1,2,0:T(8,128)(2,1)}, bf16[16,128,4,128]{3,1,2,0:T(8,128)(2,1)}, u32[]{:S(2)}, u32[]{:S(2)}) collective-permute-start(bf16[16,128,4,128]{3,1,2,0:T(8,128)(2,1)} %get-tuple-element.1318), channel_id=1, source_target_pairs={{0,1},{1,2},{2,3},{3,4},{4,5},{5,6},{6,7},{7,0},{8,9},{9,10},{10,1... | collective-permute-start | bytes 6291464 | tf_op jit(solution)/shard_map/while/body/eval_jaxpr/ppermute | solution.py:123
  3486.1 287.7 %collective-permute-start.6 = (f32[16,128,4,128]{1,0,3,2:T(8,128)}, f32[16,128,4,128]{1,0,3,2:T(8,128)}, u32[]{:S(2)}, u32[]{:S(2)}) collective-permute-start(f32[16,128,4,128]{1,0,3,2:T(8,128)} %copy.56), channel_id=1, source_target_pairs={{0,1},{1,2},{2,3},{3,4},{4,5},{5,6},{6,7},{7,0},{8,9},{9,10},{10,1... | collective-permute-start | bytes 12582920 | tf_op jit(solution)/shard_map/ppermute | solution.py:147
  3493.2 280.6 %collective-permute-start.7 = (bf16[16,128,4,128]{3,2,1,0:T(4,128)(2,1)S(1)}, bf16[16,128,4,128]{3,2,1,0:T(4,128)(2,1)}, u32[]{:S(2)}, u32[]{:S(2)}) collective-permute-start(bf16[16,128,4,128]{3,2,1,0:T(4,128)(2,1)S(1)} %copy.57), channel_id=1, source_target_pairs={{0,1},{1,2},{2,3},{3,4},{4,5},{5,6},{6,7},{7,0},{8,9},{9,10},{10,1... | collective-permute-start | bytes 6291464 | tf_op jit(solution)/shard_map/ppermute | solution.py:147
  3676.8 32.9 copy-start.23
  (67 other events, 994.3 us)
where the time goes:
time: 3800 us; the launch traced here: 3780 us
  matrix products  1440 us (38%)
  waiting for transfers between devices  1070 us (28%)
  starting transfers between devices  494 us (13%)
  local copies, waits for them, and re-layouts  351 us (9%)
  other arithmetic  331 us (9%)
  loops' own time  103 us (3%)
    ppermute x28, waiting for transfers between devices, backward_step(): kv_buf, dkv_buf = lax.ppermute((kv_buf, dkv_buf), 'cp', shift_pairs)  749 us
    ppermute x14, waiting for transfers between devices, forward_step(): kv_buf = lax.ppermute(kv_buf, 'cp', shift_pairs)  318 us
    ppermute x28, starting transfers between devices, backward_step(): kv_buf, dkv_buf = lax.ppermute((kv_buf, dkv_buf), 'cp', shift_pairs)  301 us
    dot_general x14, matrix products, attend_block(): jnp.einsum('bqhgd,bkhd->bhgqk', q_part, k_part, preferred_element_type=jn...  253 us
    dot_general x14, matrix products, attend_block(): jnp.einsum('bhgqk,bkhd->bhgqd', weights.astype(jnp.bfloat16), v_part, pre...  246 us
    dot_general x14, matrix products, grad_block(): jnp.einsum('bhgqk,bkhd->bhgqd', grad_scores, k_part, preferred_element_ty...  212 us
    dot_general x14, matrix products, grad_block(): jnp.einsum('bqhgd,bkhd->bhgqk', g_part, v_part, preferred_element_type=jn...  212 us
    dot_general x14, matrix products, grad_block(): jnp.einsum('bhgqk,bqhgd->bkhd', weights.astype(jnp.bfloat16), g_part, pre...  193 us
  transfers between devices with their start and end apart: 44, of which 28 were waited for; matrix products, arithmetic and copies ran while one was open for 5% of the time, Pallas kernels for 0%

commit v1 on v0

v1 whole, which is shorter than its diff:
```python
import functools

import jax
import jax.numpy as jnp
from jax import lax
from jax.experimental import pallas as pl
from jax.experimental.pallas import tpu as pltpu
from jax.sharding import PartitionSpec as P

ROPE_THETA = 1000000.0
LOG2E = 1.4426950408889634
PIECE = 64
KEY_BLOCK = 256
N_CHUNKS = 4


def rope_tables(positions, head_dim):
    half_dim = head_dim // 2
    freq_expo = jnp.arange(half_dim, dtype=jnp.float32) * (2.0 / head_dim)
    inv_freq = 1.0 / (ROPE_THETA ** freq_expo)
    angles = positions.astype(jnp.float32)[:, :, None] * inv_freq
    return jnp.cos(angles), jnp.sin(angles)


def rotary(tensor, cosine, sine_val):
    cosine = cosine[:, :, None, :]
    sine_val = sine_val[:, :, None, :]
    pairs = tensor.astype(jnp.float32).reshape(tensor.shape[:-1] + (tensor.shape[-1] // 2, 2))
    even_part = pairs[..., 0]
    odd_part = pairs[..., 1]
    new_even = even_part * cosine - odd_part * sine_val
    new_odd = even_part * sine_val + odd_part * cosine
    return jnp.stack([new_even, new_odd], axis=-1).reshape(tensor.shape)


def dot_nn(a, b):
    return jnp.dot(a, b, preferred_element_type=jnp.float32)


def dot_nt(a, b):
    return lax.dot_general(a, b, (((1,), (1,)), ((), ())), preferred_element_type=jnp.float32)


def swap_pairs(x):
    lane = lax.broadcasted_iota(jnp.int32, x.shape, 1)
    return jnp.where(lane % 2 == 0, pltpu.roll(x, x.shape[1] - 1, axis=1), pltpu.roll(x, 1, axis=1))


def unit_kernel(n_dev, rows, idx_ref, q_ref, g_ref, cos_ref, sin_ref, kv_ref, o_in, dq_in,
                o_ref, dq_ref, dkv_ref,
                cosb, sinb, qr, gs, ks, vs, kt, vt, dk, dv, s_ref, o_t, dq_t):
    del o_in, dq_in
    tokens, group, dim = q_ref.shape[1:]
    total = tokens * group
    half = dim // 2
    scale = dim ** -0.5
    c1 = scale * LOG2E
    me = idx_ref[0]
    n_pieces = 2 * n_dev
    per_block = KEY_BLOCK // PIECE

    @pl.when(pl.program_id(1) == 0)
    def _():
        cosb[...] = jnp.broadcast_to(cos_ref[0][:, None, :], cosb.shape)
        sinb[...] = jnp.broadcast_to(sin_ref[0][:, None, :], sinb.shape)

    cos_rows = cosb[...].reshape(total, dim)
    sin_rows = sinb[...].reshape(total, dim)
    x = q_ref[0].astype(jnp.float32).reshape(total, dim)
    qr[...] = (x * cos_rows + swap_pairs(x) * sin_rows).astype(jnp.bfloat16)
    gs[...] = g_ref[0].astype(jnp.float32).reshape(total, dim).astype(jnp.bfloat16)

    for p in range(n_pieces):
        d, hf = min(p, n_pieces - 1 - p), int(p >= n_dev)
        ks[p * PIECE:(p + 1) * PIECE, :] = kv_ref[d, hf, 0, 0, 0]
        vs[p * PIECE:(p + 1) * PIECE, :] = kv_ref[d, hf, 0, 0, 1]
    eye = (lax.broadcasted_iota(jnp.int32, (dim, dim), 0) ==
           lax.broadcasted_iota(jnp.int32, (dim, dim), 1)).astype(jnp.float32).astype(jnp.bfloat16)
    n_blocks = n_pieces // per_block
    for j in range(n_blocks):
        kt[j] = dot_nt(eye, ks[j * KEY_BLOCK:(j + 1) * KEY_BLOCK, :]).astype(jnp.bfloat16)
        vt[j] = dot_nt(eye, vs[j * KEY_BLOCK:(j + 1) * KEY_BLOCK, :]).astype(jnp.bfloat16)
    dk[...] = jnp.zeros_like(dk)
    dv[...] = jnp.zeros_like(dv)

    for part in range(2):
        piece = me if part == 0 else n_pieces - 1 - me
        n_full = piece // per_block
        base = part * rows
        q_blk = qr[base:base + rows, :]
        g_blk = gs[base:base + rows, :]

        def block_ds(j):
            return pl.ds(pl.multiple_of(j * KEY_BLOCK, KEY_BLOCK), KEY_BLOCK)

        def fold_max(s):
            return jnp.max(s.reshape(KEY_BLOCK // 8, 8, rows), axis=0)

        def score_step(j, m8):
            s = dot_nt(ks[block_ds(j), :], qr[base:base + rows, :])
            s_ref[j] = s
            return jnp.maximum(m8, fold_max(s))

        m8 = lax.fori_loop(0, n_full, score_step, jnp.full((8, rows), -jnp.inf, jnp.float32))
        s = dot_nt(ks[block_ds(n_full), :], q_blk)
        key_tok = lax.broadcasted_iota(jnp.int32, s.shape, 0) + (n_full * KEY_BLOCK - piece * PIECE)
        q_tok = lax.broadcasted_iota(jnp.int32, s.shape, 1) // group
        s = jnp.where(key_tok <= q_tok, s, -jnp.inf)
        s_ref[n_full] = s
        m8 = jnp.maximum(m8, fold_max(s))
        row_max = jnp.max(m8, axis=0, keepdims=True) * c1

        o_t[...] = jnp.zeros_like(o_t)

        def out_step(j, l8):
            p = jnp.exp2(s_ref[j] * c1 - row_max)
            o_t[...] += dot_nn(vt[j], p.astype(jnp.bfloat16))
            return l8 + jnp.sum(p.reshape(KEY_BLOCK // 8, 8, rows), axis=0)

        l8 = lax.fori_loop(0, n_full + 1, out_step, jnp.zeros((8, rows), jnp.float32))
        row_sum = jnp.sum(l8, axis=0, keepdims=True)
        out_t = o_t[...] / row_sum
        g_t = dot_nt(eye, g_blk)
        delta = jnp.sum(g_t * out_t, axis=0, keepdims=True)
        o_ref[0, part * PIECE:(part + 1) * PIECE] = jnp.transpose(out_t).reshape(PIECE, group, dim).astype(jnp.bfloat16)
        log_norm = row_max + jnp.log2(row_sum)

        dq_t[...] = jnp.zeros_like(dq_t)

        def grad_step(j, carry):
            ds_j = block_ds(j)
            p = jnp.exp2(s_ref[j] * c1 - log_norm)
            dp = dot_nt(vs[ds_j, :], gs[base:base + rows, :])
            ds = (p * (dp - delta)).astype(jnp.bfloat16)
            dv[ds_j, :] += dot_nn(p.astype(jnp.bfloat16), gs[base:base + rows, :])
            dk[ds_j, :] += dot_nn(ds, qr[base:base + rows, :])
            dq_t[...] += dot_nn(kt[j], ds)
            return carry

        lax.fori_loop(0, n_full + 1, grad_step, 0)
        dq = jnp.transpose(dq_t[...]) * scale
        cs = cosb[part * PIECE:(part + 1) * PIECE].reshape(rows, dim)
        sn = sinb[part * PIECE:(part + 1) * PIECE].reshape(rows, dim)
        dq = dq * cs - swap_pairs(dq) * sn
        dq_ref[0, part * PIECE:(part + 1) * PIECE] = dq.reshape(PIECE, group, dim).astype(jnp.bfloat16)

    for p in range(n_pieces):
        d, hf = min(p, n_pieces - 1 - p), int(p >= n_dev)
        dkv_ref[d, hf, 0, 0, 0] = dk[p * PIECE:(p + 1) * PIECE, :] * scale
        dkv_ref[d, hf, 0, 0, 1] = dv[p * PIECE:(p + 1) * PIECE, :]


def attend(idx, query, grad_out, cos_l, sin_l, kv, o_buf, dq_buf, first_batch, n_batch, n_dev):
    batch, length, n_heads, dim = query.shape
    n_kv = kv.shape[3]
    group = n_heads // n_kv
    rows = PIECE * group
    n_keys = n_dev * length
    n_blocks = n_keys // KEY_BLOCK
    head_block = pl.BlockSpec((1, length, group, dim), lambda b, h, idx: (first_batch + b, 0, h, 0))
    table_block = pl.BlockSpec((1, length, dim), lambda b, h, idx: (first_batch + b, 0, 0))
    kv_block = pl.BlockSpec((n_dev, 2, 1, 1, 2, PIECE, dim), lambda b, h, idx: (0, 0, b, h, 0, 0, 0))
    any_block = pl.BlockSpec(memory_space=pl.ANY)
    aliased = o_buf is not None
    if not aliased:
        o_buf = dq_buf = jnp.zeros((8, 128), jnp.bfloat16)
    n_elems = n_batch * n_kv * 5 * KEY_BLOCK * rows
    return pl.pallas_call(
        functools.partial(unit_kernel, n_dev, rows),
        name=f'attend_{first_batch}',
        grid_spec=pltpu.PrefetchScalarGridSpec(
            num_scalar_prefetch=1,
            grid=(n_batch, n_kv),
            in_specs=[head_block, head_block, table_block, table_block, kv_block, any_block, any_block],
            out_specs=[head_block, head_block, kv_block],
            scratch_shapes=[
                pltpu.VMEM((length, group, dim), jnp.float32),
                pltpu.VMEM((length, group, dim), jnp.float32),
                pltpu.VMEM((2 * rows, dim), jnp.bfloat16),
                pltpu.VMEM((2 * rows, dim), jnp.bfloat16),
                pltpu.VMEM((n_keys, dim), jnp.bfloat16),
                pltpu.VMEM((n_keys, dim), jnp.bfloat16),
                pltpu.VMEM((n_blocks, dim, KEY_BLOCK), jnp.bfloat16),
                pltpu.VMEM((n_blocks, dim, KEY_BLOCK), jnp.bfloat16),
                pltpu.VMEM((n_keys, dim), jnp.float32),
                pltpu.VMEM((n_keys, dim), jnp.float32),
                pltpu.VMEM((n_blocks, KEY_BLOCK, rows), jnp.float32),
                pltpu.VMEM((dim, rows), jnp.float32),
                pltpu.VMEM((dim, rows), jnp.float32),
            ]),
        out_shape=[
            jax.ShapeDtypeStruct(query.shape, jnp.bfloat16),
            jax.ShapeDtypeStruct(query.shape, jnp.bfloat16),
            jax.ShapeDtypeStruct(kv.shape, jnp.float32),
        ],
        input_output_aliases={6: 0, 7: 1} if aliased else {},
        cost_estimate=pl.CostEstimate(
            flops=12 * n_elems * dim, transcendentals=2 * n_elems,
            bytes_accessed=n_batch * (query.size // batch) * 8 + kv.size * 6),
        compiler_params=pltpu.CompilerParams(
            dimension_semantics=('arbitrary', 'arbitrary'), vmem_limit_bytes=48 * 1024 * 1024),
    )(idx, query, grad_out, cos_l, sin_l, kv, o_buf, dq_buf)


def solution(mesh):
    n_dev = mesh.shape['cp']
    head_spec = P(None, 'cp', 'tp', None)
    pos_spec = P(None, 'cp')

    def local_step(query, keys, values, positions, grad_out):
        batch, length, n_heads, dim = query.shape
        n_kv = keys.shape[2]
        cosine, sine_val = rope_tables(positions, dim)
        k_rot = rotary(keys, cosine, sine_val).astype(jnp.bfloat16)

        def by_piece(tensor):
            return tensor.reshape(batch, 2, PIECE, n_kv, dim).transpose(1, 0, 3, 2, 4)

        kv_own = jnp.stack([by_piece(k_rot), by_piece(values)], axis=3)
        cos_l = jnp.repeat(cosine, 2, axis=-1)
        sin_l = jnp.stack([-sine_val, sine_val], axis=-1).reshape(batch, length, dim)
        idx = lax.axis_index('cp').astype(jnp.int32).reshape(1)

        n_batch = batch // N_CHUNKS
        gathered = [lax.all_gather(kv_own[:, c * n_batch:(c + 1) * n_batch], 'cp') for c in range(N_CHUNKS)]
        o_buf = dq_buf = None
        sums = []
        for c in range(N_CHUNKS):
            o_buf, dq_buf, dkv = attend(idx, query, grad_out, cos_l, sin_l, gathered[c], o_buf, dq_buf,
                                        c * n_batch, n_batch, n_dev)
            sums.append(lax.psum_scatter(dkv, 'cp', scatter_dimension=0, tiled=False))
        dkv_sum = jnp.concatenate(sums, axis=1)

        def from_piece(tensor):
            return tensor.transpose(1, 0, 3, 2, 4).reshape(batch, length, n_kv, dim)

        grad_keys = rotary(from_piece(dkv_sum[:, :, :, 0]), cosine, -sine_val).astype(jnp.bfloat16)
        grad_values = from_piece(dkv_sum[:, :, :, 1]).astype(jnp.bfloat16)
        return o_buf, dq_buf, grad_keys, grad_values

    return jax.shard_map(local_step, mesh=mesh,
                         in_specs=(head_spec, head_spec, head_spec, pos_spec, head_spec),
                         out_specs=(head_spec, head_spec, head_spec, head_spec), check_vma=False)
```

time: 3800 us -> 761 us (0.20)
  matrix products: 1440 us -> 0 us
  waiting for transfers between devices: 1070 us -> 245 us
  starting transfers between devices: 494 us -> 0.73 us
  Pallas kernels: 0 us -> 393 us
  other arithmetic: 331 us -> 30.5 us
  local copies, waits for them, and re-layouts: 351 us -> 73.3 us
  loops' own time: 103 us -> 0 us
    dot_general x96 -> x0, matrix products: 1440 us -> none  [the longest x14 253 us: attend_block(): jnp.einsum('bqhgd,bkhd->bhgqk', q_part, k_part, preferred_element_type=jn...]
    ppermute x44 -> x0, waiting for transfers between devices: 1070 us -> none  [the longest x28 749 us: backward_step(): kv_buf, dkv_buf = lax.ppermute((kv_buf, dkv_buf), 'cp', shift_pairs)]
    ppermute x44 -> x0, starting transfers between devices: 494 us -> none  [the longest x28 301 us: backward_step(): kv_buf, dkv_buf = lax.ppermute((kv_buf, dkv_buf), 'cp', shift_pairs)]
    pallas_call x0 -> x4, Pallas kernels: none -> 393 us  [attend(): pl.pallas_call(functools.partial(unit_kernel, n_dev, rows), name=f'attend...]
    reduce_scatter x0 -> x4, waiting for transfers between devices: none -> 215 us  [local_step(): sums.append(lax.psum_scatter(dkv, 'cp', scatter_dimension=0, tiled=False))]
    reduce_sum x14 -> x0, other arithmetic: 154 us -> none  [attend_block(): row_sum = row_sum * factor + jnp.sum(weights, axis=-1)]
    while x41 -> x0, local copies, waits for them, and re-layouts: 142 us -> none  [the longest x4 71.4 us: local_step(): lax.fori_loop(1, cp_size, backward_step, ((k_rot, values), (dk_acc, dv_ac...]
    unnamed x59 -> x3, local copies, waits for them, and re-layouts: 134 us -> 9.01 us
  transfers between devices with their start and end apart: 44 -> 8, of which waited for: 28 -> 3; matrix products, arithmetic and copies ran while one was open for 5% -> 3% of each run, Pallas kernels for 0% -> 52%
where the time goes in v1:
time: 761 us; the launch traced here: 758 us
  Pallas kernels  393 us (52%)
  waiting for transfers between devices  245 us (32%)
  local copies, waits for them, and re-layouts  73.3 us (10%)
  other arithmetic  30.5 us (4%)
  between operations  14.3 us (2%)
    pallas_call x4, Pallas kernels, attend(): pl.pallas_call(functools.partial(unit_kernel, n_dev, rows), name=f'attend...  393 us
    reduce_scatter x4, waiting for transfers between devices, local_step(): sums.append(lax.psum_scatter(dkv, 'cp', scatter_dimension=0, tiled=False))  215 us
    all_gather x4, waiting for transfers between devices, local_step(): lax.all_gather(kv_own[:, c * n_batch:(c + 1) * n_batch], 'cp')  29.9 us
    slice x4, local copies, waits for them, and re-layouts, local_step(): kv_own[:, c * n_batch:(c + 1) * n_batch]  22 us
    another operation x1, other arithmetic, local_step(): kv_own = jnp.stack([by_piece(k_rot), by_piece(values)], axis=3)  17.7 us
  transfers between devices with their start and end apart: 8, of which 3 were waited for; matrix products, arithmetic and copies ran while one was open for 3% of the time, Pallas kernels for 52%

profile of v1, /device:TPU:13, one launch (start us, length us, event | category | flops | bytes accessed | tf_op | source)
XLA Modules:
  0.0 757.6 jit_solution(3811298990226881755)
XLA Ops:
  7.2 0.0 all-gather.15.cloned.1.call-start
  7.2 0.7 convert_element_type.23
  7.9 3.0 copy.53
  11.0 0.6 convert.21
  11.6 1.9 fusion.5
  13.5 0.5 subtract_convert_fusion.1
  14.0 0.2 pad_maximum_fusion.2
  14.2 3.3 convert_element_type.24
  17.5 11.6 %copy.55 = bf16[16,2,64,4,128]{2,1,0,4,3:T(2,128)(2,1)} copy(bf16[16,2,64,4,128]{4,3,2,1,0:T(4,128)(2,1)} %bitcast.46) | data formatting | bytes 4194304 | tf_op jit(solution)/shard_map/reshape | solution.py:217
  29.1 17.7 %pad_maximum_fusion.1 = (bf16[2,4,4,2,64,128]{4,0,1,5,2,3:T(2,128)(2,1)}, bf16[2,4,4,2,64,128]{4,0,1,5,2,3:T(2,128)(2,1)S(1)}, bf16[2,4,4,2,64,128]{4,0,1,5,2,3:T(2,128)(2,1)}, bf16[2,4,4,2,64,128]{4,0,1,5,2,3:T(2,128)(2,1)}) fusion(bf16[2,16,4,1,64,128]{4,0,1,5,2,3:T(2,128)(2,1)} %bitcast.37, bf16[2,16,4,1,64,128]{4,0,1,5,2,3:T(2,128)(2,1)} %bitcast.36), kind=kLoop, calls=%fused_computation.13 | loop fusion | flops 2097152 | bytes 8388608 | tf_op jit(solution)/shard_map/stack | solution.py:219
  46.8 5.9 copy.59
  52.7 0.0 all-gather.13.cloned.1.call-start
  52.7 5.9 copy.58
  58.6 0.0 all-gather.11.cloned.1.call-start
  58.7 5.9 copy.57
  64.6 0.0 all-gather.9.cloned.1.call-start
  64.7 4.3 copy.56
  69.0 0.2 reduce-scatter.5.cloned.1.call-start
  69.2 1.8 fusion.4
  71.0 0.1 pad_maximum_fusion.4
  71.1 0.4 copy.67.sin_ref
  71.5 1.1 broadcast_in_dim.4
  72.6 1.6 copy.66.cos_ref
  74.2 29.8 %all-gather.15.cloned.1.call-done = bf16[16,4,4,2,64,128]{5,4,3,2,1,0:T(8,128)(2,1)} async-done(((bf16[2,4,4,2,64,128]{5,4,3,2,1,0:T(8,128)(2,1)}), bf16[16,4,4,2,64,128]{5,4,3,2,1,0:T(8,128)(2,1)}) %all-gather.15.cloned.1.call-update) | async-done | bytes 8388624 | tf_op jit(solution)/shard_map/all_gather | solution.py:225
  104.0 98.2 %attend_0.1 = (bf16[16,128,32,128]{3,2,1,0:T(8,128)(2,1)}, bf16[16,128,32,128]{3,2,1,0:T(8,128)(2,1)}, f32[8,2,4,4,2,64,128]{6,5,4,3,2,1,0:T(8,128)}) custom-call(s32[1]{0:T(128)} %bitcast.idx_ref, bf16[16,128,32,128]{3,2,1,0:T(8,128)(2,1)} %q_ref.7, bf16[16,128,32,128]{3,2,1,0:T(8,128)(2,1)} %g_ref.7, f32[16,128,128]{2,1,0:T(8,128)S(1)} %copy.66.cos_ref, ...), custom_call_target="tpu_custom_call" | custom-call | flops 16106127360 | bytes 41943040 | tf_op jit(solution)/shard_map/attend_0/pallas_call | solution.py:168
  202.2 0.0 reduce-scatter.7.cloned.1.call-start
  202.3 0.0 all-gather.13.cloned.1.call-done
  202.3 98.4 %attend_4.1 = (bf16[16,128,32,128]{3,2,1,0:T(8,128)(2,1)}, bf16[16,128,32,128]{3,2,1,0:T(8,128)(2,1)}, f32[8,2,4,4,2,64,128]{6,5,4,3,2,1,0:T(8,128)}) custom-call(s32[1]{0:T(128)} %bitcast.idx_ref, bf16[16,128,32,128]{3,2,1,0:T(8,128)(2,1)} %q_ref.7, bf16[16,128,32,128]{3,2,1,0:T(8,128)(2,1)} %g_ref.7, ...), custom_call_target="tpu_custom_call", output_to_operand_aliasing={{0}: (6, {}), {1}: (7, {})} | custom-call | flops 16106127360 | bytes 41943040 | tf_op jit(solution)/shard_map/attend_4/pallas_call | solution.py:168
  300.7 0.0 reduce-scatter.9.cloned.1.call-start
  300.8 0.0 all-gather.11.cloned.1.call-done
  300.8 98.4 %attend_8.1 = (bf16[16,128,32,128]{3,2,1,0:T(8,128)(2,1)}, bf16[16,128,32,128]{3,2,1,0:T(8,128)(2,1)}, f32[8,2,4,4,2,64,128]{6,5,4,3,2,1,0:T(8,128)}) custom-call(s32[1]{0:T(128)} %bitcast.idx_ref, bf16[16,128,32,128]{3,2,1,0:T(8,128)(2,1)} %q_ref.7, bf16[16,128,32,128]{3,2,1,0:T(8,128)(2,1)} %g_ref.7, ...), custom_call_target="tpu_custom_call", output_to_operand_aliasing={{0}: (6, {}), {1}: (7, {})} | custom-call | flops 16106127360 | bytes 41943040 | tf_op jit(solution)/shard_map/attend_8/pallas_call | solution.py:168
  399.2 0.3 reduce-scatter.11.cloned.1.call-start
  399.5 0.0 all-gather.9.cloned.1.call-done
  399.5 98.4 %attend_12.1 = (bf16[16,128,32,128]{3,2,1,0:T(8,128)(2,1)}, bf16[16,128,32,128]{3,2,1,0:T(8,128)(2,1)}, f32[8,2,4,4,2,64,128]{6,5,4,3,2,1,0:T(8,128)}) custom-call(s32[1]{0:T(128)} %bitcast.idx_ref, bf16[16,128,32,128]{3,2,1,0:T(8,128)(2,1)} %q_ref.7, bf16[16,128,32,128]{3,2,1,0:T(8,128)(2,1)} %g_ref.7, ...), custom_call_target="tpu_custom_call", output_to_operand_aliasing={{0}: (6, {}), {1}: (7, {})} | custom-call | flops 16106127360 | bytes 41943040 | tf_op jit(solution)/shard_map/attend_12/pallas_call | solution.py:168
  497.9 0.0 reduce-scatter.5.cloned.1.call-done
  498.0 0.0 reduce-scatter.7.cloned.1.call-done
  498.0 102.1 %reduce-scatter.9.cloned.1.call-done = f32[1,2,4,4,2,64,128]{6,5,4,3,2,1,0:T(8,128)} async-done(((f32[8,2,4,4,2,64,128]{6,5,4,3,2,1,0:T(8,128)}), f32[1,2,4,4,2,64,128]{6,5,4,3,2,1,0:T(8,128)}) %reduce-scatter.9.cloned.1.call-update) | async-done | bytes 2097168 | tf_op jit(solution)/shard_map/reduce_scatter | solution.py:231
  600.1 113.2 %reduce-scatter.11.cloned.1.call-done = f32[1,2,4,4,2,64,128]{6,5,4,3,2,1,0:T(8,128)} async-done(((f32[8,2,4,4,2,64,128]{6,5,4,3,2,1,0:T(8,128)}), f32[1,2,4,4,2,64,128]{6,5,4,3,2,1,0:T(8,128)}) %reduce-scatter.11.cloned.1.call-update) | async-done | bytes 2097168 | tf_op jit(solution)/shard_map/reduce_scatter | solution.py:231
  713.3 4.0 pad_maximum_fusion
  717.3 0.5 fusion.3
  717.8 2.6 slice_bitcast_fusion
  720.4 0.2 copy.69
  720.6 3.1 copy.71
  723.7 12.2 %copy.68 = f32[16,2,64,4,128]{2,1,0,4,3:T(2,128)} copy(f32[16,2,64,4,128]{4,2,3,0,1:T(8,128)} %slice_bitcast_fusion) | data formatting | bytes 8388608 | tf_op jit(solution)/shard_map/transpose | solution.py:235
  736.0 8.8 %reshape_reshape.3 = f32[16,128,4,64,2]{1,0,4,3,2:T(8,128)} reshape(f32[16,2,64,4,128]{2,1,0,4,3:T(2,128)} %copy.68) | data formatting | bytes 8388608 | tf_op jit(solution)/shard_map/reshape;reshape | solution.py:28
  744.8 2.8 subtract_convert_fusion
  747.6 0.2 pad_maximum_fusion.3
  747.8 2.9 copy.70
  (10 shorter events, 0.1 us)
Async XLA Ops:
  7.2 96.8 %all-gather.15.cloned.1.call-start = ((), (), s32[]{:S(2)}) async-start(), calls=%async_computation.11 | async-start | bytes 9437184 | tf_op jit(solution)/shard_map/all_gather | solution.py:225
  52.7 149.6 %all-gather.13.cloned.1.call-start = ((), (), s32[]{:S(2)}) async-start(), calls=%async_computation.10 | async-start | bytes 9437184 | tf_op jit(solution)/shard_map/all_gather | solution.py:225
  58.6 242.1 %all-gather.11.cloned.1.call-start = ((), (), s32[]{:S(2)}) async-start(), calls=%async_computation.9 | async-start | bytes 9437184 | tf_op jit(solution)/shard_map/all_gather | solution.py:225
  64.6 334.9 %all-gather.9.cloned.1.call-start = ((), (), s32[]{:S(2)}) async-start(), calls=%async_computation.8 | async-start | bytes 9437184 | tf_op jit(solution)/shard_map/all_gather | solution.py:225
  69.0 429.0 %reduce-scatter.5.cloned.1.call-start = ((), (), s32[]{:S(2)}) async-start(), calls=%async_computation.4 | async-start | bytes 18874368 | tf_op jit(solution)/shard_map/reduce_scatter | solution.py:231
  202.2 295.8 %reduce-scatter.7.cloned.1.call-start = ((), (), s32[]{:S(2)}) async-start(), calls=%async_computation.5 | async-start | bytes 18874368 | tf_op jit(solution)/shard_map/reduce_scatter | solution.py:231
  300.7 299.4 %reduce-scatter.9.cloned.1.call-start = ((), (), s32[]{:S(2)}) async-start(), calls=%async_computation.6 | async-start | bytes 18874368 | tf_op jit(solution)/shard_map/reduce_scatter | solution.py:231
  399.2 314.1 %reduce-scatter.11.cloned.1.call-start = ((), (), s32[]{:S(2)}) async-start(), calls=%async_computation.7 | async-start | bytes 18874368 | tf_op jit(solution)/shard_map/reduce_scatter | solution.py:231
Sparse Core Ops, SparseCore 0:
  52.8 51.1 all-gather.14
  105.8 50.1 all-gather.12
  157.9 50.2 all-gather.10
  210.4 50.3 all-gather.8
  264.2 109.5 reduce-scatter.4
  377.2 109.6 reduce-scatter.6
  490.4 109.7 reduce-scatter.8
  603.6 109.6 reduce-scatter.10
